TPU v7x, 256 devices: a 4x2x16 block of a 4x16x16 slice. The times are simulated.
256 devices in a mesh: groups: 2 (over y), freq: 128 (over z, x, core).
Axes of the slice: x: 4, y: 2, z: 16, core: 2. Of those that a mesh axis runs over, the one named last changes fastest.
The devices are a block of a 4x16x16 slice.
Arguments:
- primary_one: bfloat16 [1024, 512, 512], P(('groups', 'freq')), parts along dimension 0, may hold values from -6 to 6
- primary_two: bfloat16 [1024, 512, 512], P(('groups', 'freq')), parts along dimension 0, may hold values from -6 to 6
- primary_three: bfloat16 [1024, 512, 512], P(('groups', 'freq')), parts along dimension 0, may hold values from -6 to 6
- window_start: int32 [3, 1024, 512], P(None, ('groups', 'freq')), parts along dimension 1, may hold values from 0 to 255
- window_end: int32 [3, 1024, 512], P(None, ('groups', 'freq')), parts along dimension 1, may hold values from 257 to 512
Outputs:
- predicted: bfloat16 [1024, 512, 512], P(('groups', 'freq')), parts along dimension 0
There are 2 independent parts, one for each index of `groups`. A program takes and returns all parts, laid end to end along the dimension named above; each array names one. Nothing has to cross between parts.
Inputs may be any that keep to these rules, and one draw needn't show every extreme that they name: window_start of a trace is below its window_end.
All inputs are finite; a program needn't handle non-finite values.
Results may differ from a plain program's by a relative error of at most 0.0089.
Values may be sent and summed in bfloat16 or wider, within the bound.
A program may use at most 64 MiB of HBM per device.

v0:
```python
import jax
import jax.numpy as jnp
from jax import lax
from jax.sharding import PartitionSpec as P

F_DEV = 1


def sent_together(arrays, axis, split_dim, concat_dim, along):
    widths = [a.shape[along] for a in arrays]
    both = jnp.concatenate(arrays, axis=along)
    whole = lax.all_to_all(both, axis, split_axis=split_dim, concat_axis=concat_dim, tiled=True)
    return tuple(jnp.split(whole, [sum(widths[:k]) for k in range(1, len(widths))], axis=along))


def make_table(count, samples):
    waves = jnp.arange(1, count + 1, dtype=jnp.int32)[:, None]
    times = jnp.arange(samples, dtype=jnp.int32)[None, :]
    phase = waves * times % samples
    angle = 2.0 * jnp.pi / samples * phase.astype(jnp.float32)
    both = jnp.stack([jnp.cos(angle), -jnp.sin(angle)], axis=1)
    return both.reshape(2 * count, samples).astype(jnp.bfloat16)


def spectrum(traces, start, finish, table, count):
    sources, receivers, samples = traces.shape
    times = jnp.arange(samples, dtype=jnp.int32)
    inside = (times >= start[:, :, None]) & (times < finish[:, :, None])
    windowed = jnp.where(inside, traces, jnp.zeros_like(traces))
    flat = windowed.reshape(sources * receivers, samples)
    spec = lax.dot_general(
        table, flat, (((1,), (1,)), ((), ())), preferred_element_type=jnp.float32
    )
    spec = spec * (1.0 / jnp.sqrt(jnp.float32(samples)))
    return spec.astype(jnp.bfloat16).reshape(count, 2, sources, receivers)


def correlate(first, second):
    swapped = jnp.stack([first[:, 1], -first[:, 0]], axis=1)
    left = jnp.stack([first, swapped], axis=1)
    cross = jnp.einsum("fkcsr,fcur->fksu", left, second, preferred_element_type=jnp.float32)
    cross = cross * (1.0 / jnp.sqrt(jnp.float32(first.shape[3])))
    return cross.astype(jnp.bfloat16)


def convolve(cross, third):
    right = jnp.stack(
        [
            jnp.stack([third[:, 0], -third[:, 1]], axis=1),
            jnp.stack([third[:, 1], third[:, 0]], axis=1),
        ],
        axis=1,
    )
    multiple = jnp.einsum("fcsu,fkcur->fksr", cross, right, preferred_element_type=jnp.float32)
    multiple = multiple * (1.0 / jnp.sqrt(jnp.float32(third.shape[2])))
    return multiple.astype(jnp.bfloat16)


def on_device(primary_one, primary_two, primary_three, window_start, window_end):
    samples = primary_one.shape[2]
    count = F_DEV * lax.axis_size("freq")
    table = make_table(count, samples)
    spec_one = spectrum(primary_one, window_start[0], window_end[0], table, count)
    spec_two = spectrum(primary_two, window_start[1], window_end[1], table, count)
    spec_three = spectrum(primary_three, window_start[2], window_end[2], table, count)
    first, second = sent_together((spec_one, spec_two), "freq", 0, 2, 1)
    cross = correlate(first, second)
    third = lax.all_to_all(spec_three, "freq", split_axis=0, concat_axis=2, tiled=True)
    multiple = convolve(cross, third)
    piece = lax.all_to_all(multiple, "freq", split_axis=2, concat_axis=0, tiled=True)
    waves, parts, sources, receivers = piece.shape
    flat = piece.reshape(waves * parts, sources * receivers)
    timed = lax.dot_general(
        flat, table, (((0,), (0,)), ((), ())), preferred_element_type=jnp.float32
    )
    timed = timed * (1.0 / jnp.sqrt(jnp.float32(count)))
    return timed.astype(jnp.bfloat16).reshape(sources, receivers, samples)


def solution(mesh):
    return jax.shard_map(
        on_device,
        mesh=mesh,
        in_specs=(
            P(("groups", "freq"), None, None),
            P(("groups", "freq"), None, None),
            P(("groups", "freq"), None, None),
            P(None, ("groups", "freq"), None),
            P(None, ("groups", "freq"), None),
        ),
        out_specs=P(("groups", "freq"), None, None),
        check_vma=False,
    )
```

profile of v0, /device:TPU:33, one launch (start us, length us, event | category | flops | bytes accessed | tf_op | source)
XLA Modules:
  0.0 281.0 jit_solution(12625566358384556773)
XLA Ops:
  0.0 0.7 slice_bitcast_fusion.3
  0.7 0.7 slice_bitcast_fusion.2
  1.5 1.2 cosine_convert_fusion
  2.7 0.3 copy.36
  3.0 0.1 convert_element_type.64
  3.1 4.2 %fusion.1 = (bf16[4,512,512]{2,1,0:T(8,128)(2,1)S(1)}, bf16[4,512,512]{2,1,0:T(8,128)(2,1)S(1)}) fusion(bf16[4,512,512]{2,1,0:T(8,128)(2,1)} %param.7, s32[4,512]{1,0:T(4,128)S(1)} %get-tuple-element.17, s32[4,512]{1,0:T(4,128)S(1)} %get-tuple-element.14, bf16[4,512,512]{2,1,0:T(8,128)(2,1)} %param.5, s32[4,512]{1,0:T(4,128)S(1)} %get-tuple-element.16, ...), kind=kLoop, calls=%fused_computation.8 | loop fusion | flops 8388608 | bytes 8421376 | tf_op jit(solution)/shard_map/jit(_where)/select_n | solution.py:29
  7.3 1.7 fusion.6
  9.0 1.8 reshape.176
  10.9 1.8 copy.37
  12.7 31.0 %all-to-all-start = ((bf16[128,2,4,512]{3,1,2,0:T(2,128)(2,1)}), bf16[128,2,4,512]{3,1,2,0:T(2,128)(2,1)S(1)}, u32[]{:S(2)}, u32[]{:S(2)}) async-start(bf16[128,2,4,512]{3,1,2,0:T(2,128)(2,1)} %copy.37), calls=%async_computation | async-start | bytes 2097152 | tf_op jit(solution)/shard_map/all_to_all | solution.py:68
  43.7 1.7 fusion.7
  45.5 1.8 reshape.179
  47.3 0.0 copy-start
  47.3 0.8 copy.40
  48.2 0.7 copy-done
  48.9 1.2 fusion.5
  50.1 1.7 fusion.8
  51.8 1.8 reshape.181
  53.7 0.8 copy.41
  54.5 3.2 %pad_maximum_fusion = bf16[128,4,4,512]{3,1,2,0:T(4,128)(2,1)} fusion(bf16[128,2,4,512]{3,1,2,0:T(2,128)(2,1)S(1)} %copy.41, bf16[128,2,4,512]{3,1,2,0:T(2,128)(2,1)S(1)} %copy.40), kind=kLoop, calls=%fused_computation.23 | loop fusion | flops 4194304 | bytes 4194304 | tf_op jit(solution)/shard_map/concatenate | solution.py:11
  57.8 36.9 %all-to-all-done = bf16[128,2,4,512]{3,1,2,0:T(2,128)(2,1)S(1)} async-done(((bf16[128,2,4,512]{3,1,2,0:T(2,128)(2,1)}), bf16[128,2,4,512]{3,1,2,0:T(2,128)(2,1)S(1)}, u32[]{:S(2)}, u32[]{:S(2)}) %all-to-all-start) | async-done | bytes 1048608 | tf_op jit(solution)/shard_map/all_to_all | solution.py:68
  94.7 11.8 %all-to-all-start.1 = ((bf16[128,4,4,512]{3,1,2,0:T(4,128)(2,1)}), bf16[128,4,4,512]{3,1,2,0:T(4,128)(2,1)S(1)}, u32[]{:S(2)}, u32[]{:S(2)}) async-start(bf16[128,4,4,512]{3,1,2,0:T(4,128)(2,1)} %pad_maximum_fusion), calls=%async_computation.1 | async-start | bytes 4194304 | tf_op jit(solution)/shard_map/all_to_all | solution.py:12
  106.5 2.5 fusion.30
  109.0 2.3 copy.51
  111.3 0.9 neg.23
  112.2 2.3 copy.50
  114.6 2.6 maximum_bitcast_fusion.12
  117.1 84.8 %all-to-all-done.1 = bf16[128,4,4,512]{3,1,2,0:T(4,128)(2,1)S(1)} async-done(((bf16[128,4,4,512]{3,1,2,0:T(4,128)(2,1)}), bf16[128,4,4,512]{3,1,2,0:T(4,128)(2,1)S(1)}, u32[]{:S(2)}, u32[]{:S(2)}) %all-to-all-start.1) | async-done | bytes 2097184 | tf_op jit(solution)/shard_map/all_to_all | solution.py:12
  202.0 1.5 fusion.29
  203.4 2.3 fusion.28
  205.7 0.1 copy.53
  205.9 0.1 copy_negate_fusion
  205.9 0.0 copy-start.1
  206.0 0.0 copy-start.2
  206.0 0.2 copy.63
  206.1 1.1 maximum_bitcast_fusion.14
  207.2 0.0 copy-done.1
  207.2 0.7 copy-done.2
  207.9 4.9 %fusion.18 = bf16[1,2,512,512]{2,3,1,0:T(8,128)(2,1)} fusion(bf16[1,1,2,512,512]{3,4,2,1,0:T(8,128)(2,1)S(1)} %copy-done.2, bf16[1,1,2,512,512]{3,4,2,1,0:T(8,128)(2,1)S(1)} %copy-done.1, bf16[1,1,2,512,512]{4,3,2,1,0:T(8,128)(2,1)} %maximum_bitcast_fusion.14, bf16[1,1,2,512,512]{4,3,2,1,0:T(8,128)(2,1)S(1)} %bitcast.104, ...), kind=kOutput, calls=%fused_computation.33 | convolution fusion | flops 2151677952 | bytes 6291456 | tf_op jit(solution)/shard_map/fcsu,fkcur->fksr/dot_general | solution.py:54
  212.8 2.5 copy.46
  215.3 63.0 %all_to_all.51 = bf16[1,2,512,512]{3,1,0,2:T(2,128)(2,1)S(1)} all-to-all(bf16[1,2,512,512]{3,1,0,2:T(2,128)(2,1)S(1)} %copy.46), channel_id=1, replica_groups=mesh['groups'=2,'freq'=128] {'freq'}, dimensions={2} | all-to-all | bytes 2097152 | tf_op jit(solution)/shard_map/all_to_all | solution.py:70
  278.2 0.4 copy.47
  278.7 0.3 copy.56
  278.9 2.1 multiply_convert_fusion
  (2 shorter events, 0.0 us)
Async XLA Ops:
  12.7 82.0 %all-to-all-start = ((bf16[128,2,4,512]{3,1,2,0:T(2,128)(2,1)}), bf16[128,2,4,512]{3,1,2,0:T(2,128)(2,1)S(1)}, u32[]{:S(2)}, u32[]{:S(2)}) async-start(bf16[128,2,4,512]{3,1,2,0:T(2,128)(2,1)} %copy.37), calls=%async_computation | async-start | bytes 2097152 | tf_op jit(solution)/shard_map/all_to_all | solution.py:68
  47.3 1.6 copy-start
  94.7 107.3 %all-to-all-start.1 = ((bf16[128,4,4,512]{3,1,2,0:T(4,128)(2,1)}), bf16[128,4,4,512]{3,1,2,0:T(4,128)(2,1)S(1)}, u32[]{:S(2)}, u32[]{:S(2)}) async-start(bf16[128,4,4,512]{3,1,2,0:T(4,128)(2,1)} %pad_maximum_fusion), calls=%async_computation.1 | async-start | bytes 4194304 | tf_op jit(solution)/shard_map/all_to_all | solution.py:12
  205.9 1.3 copy-start.1
  206.0 1.9 copy-start.2
where the time goes:
time: 284 us; the launch traced here: 281 us
  waiting for transfers between devices  122 us (43%)
  blocking collectives  63 us (22%)
  starting transfers between devices  42.8 us (15%)
  local copies, waits for them, and re-layouts  26.7 us (9%)
  other arithmetic  14.4 us (5%)
  matrix products  12.1 us (4%)
    all_to_all x1, waiting for transfers between devices, sent_together(): lax.all_to_all(both, axis, split_axis=split_dim, concat_axis=concat_dim,...  84.8 us
    all_to_all x1, blocking collectives, on_device(): lax.all_to_all(multiple, 'freq', split_axis=2, concat_axis=0, tiled=True)  63 us
    all_to_all x1, waiting for transfers between devices, on_device(): lax.all_to_all(spec_three, 'freq', split_axis=0, concat_axis=2, tiled=True)  36.9 us
    all_to_all x1, starting transfers between devices, on_device(): lax.all_to_all(spec_three, 'freq', split_axis=0, concat_axis=2, tiled=True)  31 us
    all_to_all x1, starting transfers between devices, sent_together(): lax.all_to_all(both, axis, split_axis=split_dim, concat_axis=concat_dim,...  11.8 us
    reshape x6, local copies, waits for them, and re-layouts, spectrum(): return spec.astype(jnp.bfloat16).reshape(count, 2, sources, receivers)  9.02 us
    unnamed x11, local copies, waits for them, and re-layouts  6.66 us
  transfers between devices with their start and end apart: 2, of which 2 were waited for; matrix products, arithmetic and copies ran while one was open for 8% of the time, Pallas kernels for 0%

commit v1 on v0

v1 whole, which is shorter than its diff:
```python
import functools

import jax
import jax.numpy as jnp
import numpy as np
from jax import lax
from jax.experimental import pallas as pl
from jax.experimental.pallas import tpu as pltpu
from jax.sharding import PartitionSpec as P

MESH = pl.DeviceIdType.MESH
LANES = 128
ROW = 8
F32 = jnp.float32
BF16 = jnp.bfloat16


def make_table(count, samples):
    waves = np.arange(1, count + 1, dtype=np.int64)[:, None]
    times = np.arange(samples, dtype=np.int64)[None, :]
    angle = np.float32(2.0 * np.pi / samples) * (waves * times % samples).astype(np.float32)
    both = np.concatenate([np.cos(angle), -np.sin(angle)], axis=0)
    return both.astype(BF16)


def shift_of(block):
    return ((block + 1) // 2) * (2 * (block % 2) - 1)


def kernel(
    size, p1, p2, p3, ws, we, tab_hbm, out_hbm,
    inp, wsv, wev, tab, a32, b32, s23, s1, r23, r1, xm, ym, zm, w, o, m, m32, outv,
    in_sem, out_sem, ssem23, ssem1, ssemo, rsem23, rsem1, rsemo,
):
    me = lax.axis_index("freq")
    group = lax.axis_index("groups")
    rows = size // ROW
    z, xc = me // ROW, me % ROW
    samples = tab.shape[1]
    sources, receivers = inp.shape[1], inp.shape[2]
    per = 2 * sources

    barrier = pltpu.get_barrier_semaphore()

    def greet(k, carry):
        pl.semaphore_signal(barrier, inc=1, device_id=(group, (me + k) % size), device_id_type=MESH)
        return carry

    loads = [
        pltpu.make_async_copy(ws, wsv, in_sem.at[0]),
        pltpu.make_async_copy(we, wev, in_sem.at[1]),
        pltpu.make_async_copy(tab_hbm, tab, in_sem.at[2]),
        pltpu.make_async_copy(p2, inp.at[1], in_sem.at[4]),
        pltpu.make_async_copy(p3, inp.at[2], in_sem.at[5]),
        pltpu.make_async_copy(p1, inp.at[0], in_sem.at[3]),
    ]
    for load in loads:
        load.start()
    lax.fori_loop(1, size, greet, 0)
    for load in loads[:3]:
        load.wait()

    def spectra(j, into, base, stride):
        ends = jnp.concatenate([wsv[j], wev[j]], axis=0).astype(F32)
        columns = ends.T
        times = lax.broadcasted_iota(jnp.int32, (receivers, samples), 1).astype(F32)
        for s in range(sources):
            first = columns[:, s : s + 1]
            last = columns[:, sources + s : sources + s + 1]
            inside = (times >= first) & (times < last)
            traces = jnp.where(inside, inp[j, s].astype(F32), 0.0).astype(BF16)
            spec = lax.dot_general(tab[...], traces, (((1,), (1,)), ((), ())), preferred_element_type=F32)
            spec = spec * np.float32(1.0 / np.sqrt(samples))
            for c in range(2):
                for q in range(receivers // LANES):
                    into[q, pl.ds(base + c * sources + s, size, stride=stride), :] = spec[
                        c * size : (c + 1) * size, q * LANES : (q + 1) * LANES
                    ]

    def each_partner(body):
        def step(i, carry):
            block, turn = i // ROW, i % ROW
            dst = ((z + shift_of(block) + rows) % rows) * ROW + (xc + turn) % ROW
            body(block, dst)
            return carry

        lax.fori_loop(1, size, step, 0)

    loads[3].wait()
    spectra(1, a32, 0, 2 * per)
    loads[4].wait()
    spectra(2, a32, per, 2 * per)

    def round23(i, carry):
        at = pl.multiple_of(i * ROW, ROW)
        lines = pl.ds(pl.multiple_of(i * ROW * 2 * per, ROW * 2 * per), ROW * 2 * per)
        for q in range(receivers // LANES):
            piece = a32[q, lines, :].reshape(ROW, 2 * per, LANES)
            s23[pl.ds(at, ROW), :, q * LANES : (q + 1) * LANES] = piece.astype(BF16)
        return carry

    lax.fori_loop(0, rows, round23, 0)
    pl.semaphore_wait(barrier, size - 1)

    def send23(block, dst):
        pltpu.make_async_remote_copy(
            s23.at[dst], r23.at[me], ssem23, rsem23, device_id=(group, dst), device_id_type=MESH
        ).start()

    each_partner(send23)
    r23[me] = s23[me]

    loads[5].wait()
    spectra(0, b32, 0, per)

    def round1(i, carry):
        at = pl.multiple_of(i * ROW, ROW)
        lines = pl.ds(pl.multiple_of(i * ROW * per, ROW * per), ROW * per)
        for q in range(receivers // LANES):
            piece = b32[q, lines, :].reshape(ROW, per, LANES)
            s1[pl.ds(at, ROW), :, q * LANES : (q + 1) * LANES] = piece.astype(BF16)
        return carry

    lax.fori_loop(0, rows, round1, 0)

    def send1(block, dst):
        pltpu.make_async_remote_copy(
            s1.at[dst], r1.at[me], ssem1, rsem1.at[block], device_id=(group, dst), device_id_type=MESH
        ).start()

    each_partner(send1)
    r1[me] = s1[me]

    pltpu.make_async_copy(s23.at[pl.ds(0, size - 1)], r23.at[pl.ds(0, size - 1)], rsem23).wait()
    half = lax.broadcasted_iota(jnp.int32, (ROW, per, receivers), 1)
    sign = jnp.where(half < sources, 1.0, -1.0).astype(F32)

    def arrange(i, carry):
        at = pl.multiple_of(i * ROW, ROW)
        to = pl.ds(pl.multiple_of(i * ROW * per, ROW * per), ROW * per)
        piece = r23[pl.ds(at, ROW)].astype(F32)
        second, third = piece[:, :per], piece[:, per:]
        turned = jnp.concatenate([third[:, sources:], third[:, :sources]], axis=1) * sign
        xm[to, :] = second.reshape(ROW * per, receivers).astype(BF16)
        ym[to, :] = third.reshape(ROW * per, receivers).astype(BF16)
        zm[to, :] = turned.reshape(ROW * per, receivers).astype(BF16)
        return carry

    lax.fori_loop(0, rows, arrange, 0)
    scale = np.float32(1.0 / np.sqrt(size * sources))

    def weigh(i, carry):
        at = pl.ds(pl.multiple_of(i * LANES, LANES), LANES)
        left = xm[:, at]
        dims = (((0,), (0,)), ((), ()))
        w[at, :receivers] = (lax.dot_general(left, ym[...], dims, preferred_element_type=F32) * scale).astype(BF16)
        w[at, receivers:] = (lax.dot_general(left, zm[...], dims, preferred_element_type=F32) * scale).astype(BF16)
        return carry

    lax.fori_loop(0, receivers // LANES, weigh, 0)
    scale1 = np.float32(1.0 / np.sqrt(receivers))

    def multiply(block, carry):
        came = ((z - shift_of(block) + rows) % rows) * ROW

        @pl.when(block == 0)
        def _():
            pltpu.make_async_copy(s1.at[pl.ds(0, ROW - 1)], r1.at[pl.ds(0, ROW - 1)], rsem1.at[block]).wait()

        @pl.when(block > 0)
        def _():
            pltpu.make_async_copy(s1.at[pl.ds(0, ROW)], r1.at[pl.ds(0, ROW)], rsem1.at[block]).wait()

        at = pl.ds(pl.multiple_of(came, ROW), ROW)
        piece = r1[at].astype(F32).reshape(ROW * per, receivers).astype(BF16)
        both = jnp.dot(piece, w[...], preferred_element_type=F32)
        a = both[:, :receivers].reshape(ROW, per, receivers)
        b = both[:, receivers:].reshape(ROW, per, receivers)
        turned = jnp.concatenate([b[:, sources:], b[:, :sources]], axis=1) * sign
        o[at] = ((a - turned) * scale1).astype(BF16)

        def back(turn, c):
            dst = came + (xc + turn) % ROW

            @pl.when(dst != me)
            def _():
                pltpu.make_async_remote_copy(
                    o.at[dst], m.at[me], ssemo, rsemo.at[block], device_id=(group, dst), device_id_type=MESH
                ).start()

            return c

        lax.fori_loop(0, ROW, back, 0)
        return carry

    lax.fori_loop(0, rows, multiply, 0)
    m[me] = o[me]

    def collect(block, carry):
        came = ((z + shift_of(block) + rows) % rows) * ROW

        @pl.when(block == 0)
        def _():
            pltpu.make_async_copy(o.at[pl.ds(0, ROW - 1)], m.at[pl.ds(0, ROW - 1)], rsemo.at[block]).wait()

        @pl.when(block > 0)
        def _():
            pltpu.make_async_copy(o.at[pl.ds(0, ROW)], m.at[pl.ds(0, ROW)], rsemo.at[block]).wait()

        piece = m[pl.ds(pl.multiple_of(came, ROW), ROW)].astype(F32).reshape(ROW * per, receivers)
        lines = pl.ds(pl.multiple_of(came * per, ROW * per), ROW * per)
        for q in range(receivers // LANES):
            m32[q, lines, :] = piece[:, q * LANES : (q + 1) * LANES]
        return carry

    lax.fori_loop(0, rows, collect, 0)
    scale2 = np.float32(1.0 / np.sqrt(size))
    stores = []
    for s in range(sources):
        parts = [
            jnp.concatenate([m32[q, pl.ds(c * sources + s, size, stride=per), :] for c in range(2)], axis=0)
            for q in range(receivers // LANES)
        ]
        lines = jnp.concatenate(parts, axis=1).astype(BF16)
        timed = lax.dot_general(lines, tab[...], (((0,), (0,)), ((), ())), preferred_element_type=F32)
        outv[s] = (timed * scale2).astype(BF16)
        store = pltpu.make_async_copy(outv.at[s], out_hbm.at[s], out_sem.at[s])
        store.start()
        stores.append(store)
    pltpu.make_async_copy(s23.at[pl.ds(0, size - 1)], r23.at[pl.ds(0, size - 1)], ssem23).wait()
    pltpu.make_async_copy(s1.at[pl.ds(0, size - 1)], r1.at[pl.ds(0, size - 1)], ssem1).wait()
    pltpu.make_async_copy(o.at[pl.ds(0, size - 1)], m.at[pl.ds(0, size - 1)], ssemo).wait()
    for store in stores:
        store.wait()


def on_device(size, p1, p2, p3, ws, we):
    sources, receivers, samples = p1.shape
    rows, per = size // ROW, 2 * sources
    vmem = pltpu.VMEM
    dma = pltpu.SemaphoreType.DMA
    return pl.pallas_call(
        functools.partial(kernel, size),
        out_shape=jax.ShapeDtypeStruct(p1.shape, BF16),
        in_specs=[pl.BlockSpec(memory_space=pl.ANY)] * 6,
        out_specs=pl.BlockSpec(memory_space=pl.ANY),
        scratch_shapes=[
            vmem((3,) + p1.shape, BF16),
            vmem(ws.shape, jnp.int32),
            vmem(we.shape, jnp.int32),
            vmem((2 * size, samples), BF16),
            vmem((receivers // LANES, 2 * per * size, LANES), F32),
            vmem((receivers // LANES, per * size, LANES), F32),
            vmem((size, 2 * per, receivers), BF16),
            vmem((size, per, receivers), BF16),
            vmem((size, 2 * per, receivers), BF16),
            vmem((size, per, receivers), BF16),
            vmem((size * per, receivers), BF16),
            vmem((size * per, receivers), BF16),
            vmem((size * per, receivers), BF16),
            vmem((receivers, 2 * receivers), BF16),
            vmem((size, per, receivers), BF16),
            vmem((size, per, receivers), BF16),
            vmem((receivers // LANES, size * per, LANES), F32),
            vmem(p1.shape, BF16),
            dma((6,)), dma((sources,)), dma, dma, dma, dma, dma((rows,)), dma((rows,)),
        ],
        compiler_params=pltpu.CompilerParams(
            collective_id=0, has_side_effects=True, vmem_limit_bytes=60 * 2**20
        ),
    )(p1, p2, p3, ws, we, jnp.asarray(make_table(size, samples)))


def solution(mesh):
    size = mesh.shape["freq"]
    spec = P(("groups", "freq"), None, None)
    wspec = P(None, ("groups", "freq"), None)
    return jax.shard_map(
        functools.partial(on_device, size),
        mesh=mesh,
        in_specs=(spec, spec, spec, wspec, wspec),
        out_specs=spec,
        check_vma=False,
    )
```

time: 284 us -> 221 us (0.78); the launches traced: 281 us -> 221 us
  Pallas kernels: 0 us -> 218 us
  waiting for transfers between devices: 122 us -> 0 us
  blocking collectives: 63 us -> 0 us
  starting transfers between devices: 42.8 us -> 0 us
  local copies, waits for them, and re-layouts: 26.7 us -> 3.05 us
  other arithmetic: 14.4 us -> 0 us
  matrix products: 12.1 us -> 0 us
    pallas_call x0 -> x1, Pallas kernels: none -> 218 us  [on_device(): pl.pallas_call(functools.partial(kernel, size), out_shape=jax.ShapeDtypeS...]
    all_to_all x2 -> x0, waiting for transfers between devices: 122 us -> none  [the longest x1 84.8 us: sent_together(): lax.all_to_all(both, axis, split_axis=split_dim, concat_axis=concat_dim,...]
    all_to_all x1 -> x0, blocking collectives: 63 us -> none  [on_device(): lax.all_to_all(multiple, 'freq', split_axis=2, concat_axis=0, tiled=True)]
    all_to_all x2 -> x0, starting transfers between devices: 42.8 us -> none  [the longest x1 31 us: on_device(): lax.all_to_all(spec_three, 'freq', split_axis=0, concat_axis=2, tiled=True)]
    dot_general x5 -> x0, matrix products: 12.1 us -> none  [the longest x3 5.15 us: spectrum(): lax.dot_general(table, flat, (((1,), (1,)), ((), ())), preferred_element_...]
    reshape x6 -> x0, local copies, waits for them, and re-layouts: 9.02 us -> none  [spectrum(): return spec.astype(jnp.bfloat16).reshape(count, 2, sources, receivers)]
    select_n x2 -> x0, other arithmetic: 5.4 us -> none  [spectrum(): windowed = jnp.where(inside, traces, jnp.zeros_like(traces))]
    another operation x4 -> x0, other arithmetic: 4.88 us -> none  [the longest x1 2.56 us: convolve(): jnp.stack([jnp.stack([third[:, 0], -third[:, 1]], axis=1), jnp.stack([thi...]
  transfers between devices with their start and end apart: 2 -> 0, of which waited for: 2 -> 0; matrix products, arithmetic and copies ran while one was open for 8% -> 0% of each run, Pallas kernels for 0% -> 0%
where the time goes in v1:
time: 221 us
  Pallas kernels  218 us (99%)
  local copies, waits for them, and re-layouts  3.05 us (1%)
    pallas_call x1, Pallas kernels, on_device(): pl.pallas_call(functools.partial(kernel, size), out_shape=jax.ShapeDtypeS...  218 us

profile of v1, /device:TPU:33, one launch (start us, length us, event | category | flops | bytes accessed | tf_op | source)
XLA Modules:
  0.0 220.9 jit_solution(4322350184911905844)
XLA Ops:
  0.0 217.9 %shard_map.64 = bf16[4,512,512]{2,1,0:T(8,128)(2,1)} custom-call(bf16[4,512,512]{2,1,0:T(8,128)(2,1)} %p1.1, bf16[4,512,512]{2,1,0:T(8,128)(2,1)} %p2.1, bf16[4,512,512]{2,1,0:T(8,128)(2,1)} %p3.1, s32[3,4,512]{2,1,0:T(4,128)} %ws.1, s32[3,4,512]{2,1,0:T(4,128)} %we.1, bf16[256,512]{1,0:T(8,128)(2,1)} %constant.2.clone.tab_hbm), custom_call_target="tpu_custom_call" | custom-call | tf_op jit(solution)/shard_map/pallas_call | solution.py:242
  217.9 3.0 %copy.8 = bf16[4,512,512]{2,1,0:T(8,128)(2,1)} copy(bf16[4,512,512]{2,1,0:T(8,128)(2,1)} %shard_map.64) | data formatting | bytes 4194304

commit v2 on v1

--- a/solution.py
+++ b/solution.py
@@ -28,9 +28,9 @@
 
 
 def kernel(
-    size, p1, p2, p3, ws, we, tab_hbm, out_hbm,
-    inp, wsv, wev, tab, a32, b32, s23, s1, r23, r1, xm, ym, zm, w, o, m, m32, outv,
-    in_sem, out_sem, ssem23, ssem1, ssemo, rsem23, rsem1, rsemo,
+    size, p1, p2, p3, ws, we, tab_hbm, m32, tab,
+    inp, wsv, wev, a32, b32, s23, s1, r23, r1, xm, ym, zm, w, o, m,
+    in_sem, ssem23, ssem1, ssemo, rsem23, rsem1, rsemo,
 ):
     me = lax.axis_index("freq")
     group = lax.axis_index("groups")
@@ -214,6 +214,14 @@
         return carry
 
     lax.fori_loop(0, rows, collect, 0)
+    pltpu.make_async_copy(s23.at[pl.ds(0, size - 1)], r23.at[pl.ds(0, size - 1)], ssem23).wait()
+    pltpu.make_async_copy(s1.at[pl.ds(0, size - 1)], r1.at[pl.ds(0, size - 1)], ssem1).wait()
+    pltpu.make_async_copy(o.at[pl.ds(0, size - 1)], m.at[pl.ds(0, size - 1)], ssemo).wait()
+
+
+def finish(size, m32, tab, out_hbm, outv, out_sem):
+    sources, receivers = outv.shape[0], outv.shape[1]
+    per = 2 * sources
     scale2 = np.float32(1.0 / np.sqrt(size))
     stores = []
     for s in range(sources):
@@ -227,9 +235,6 @@
         store = pltpu.make_async_copy(outv.at[s], out_hbm.at[s], out_sem.at[s])
         store.start()
         stores.append(store)
-    pltpu.make_async_copy(s23.at[pl.ds(0, size - 1)], r23.at[pl.ds(0, size - 1)], ssem23).wait()
-    pltpu.make_async_copy(s1.at[pl.ds(0, size - 1)], r1.at[pl.ds(0, size - 1)], ssem1).wait()
-    pltpu.make_async_copy(o.at[pl.ds(0, size - 1)], m.at[pl.ds(0, size - 1)], ssemo).wait()
     for store in stores:
         store.wait()
 
@@ -239,16 +244,19 @@
     rows, per = size // ROW, 2 * sources
     vmem = pltpu.VMEM
     dma = pltpu.SemaphoreType.DMA
-    return pl.pallas_call(
+    table = jnp.asarray(make_table(size, samples))
+    lines, kept = pl.pallas_call(
         functools.partial(kernel, size),
-        out_shape=jax.ShapeDtypeStruct(p1.shape, BF16),
-        in_specs=[pl.BlockSpec(memory_space=pl.ANY)] * 6,
-        out_specs=pl.BlockSpec(memory_space=pl.ANY),
+        out_shape=(
+            jax.ShapeDtypeStruct((receivers // LANES, size * per, LANES), F32),
+            jax.ShapeDtypeStruct(table.shape, BF16),
+        ),
+        in_specs=[pl.BlockSpec(memory_space=pltpu.HBM)] * 6,
+        out_specs=[pl.BlockSpec(memory_space=pltpu.VMEM)] * 2,
         scratch_shapes=[
             vmem((3,) + p1.shape, BF16),
             vmem(ws.shape, jnp.int32),
             vmem(we.shape, jnp.int32),
-            vmem((2 * size, samples), BF16),
             vmem((receivers // LANES, 2 * per * size, LANES), F32),
             vmem((receivers // LANES, per * size, LANES), F32),
             vmem((size, 2 * per, receivers), BF16),
@@ -261,14 +269,20 @@
             vmem((receivers, 2 * receivers), BF16),
             vmem((size, per, receivers), BF16),
             vmem((size, per, receivers), BF16),
-            vmem((receivers // LANES, size * per, LANES), F32),
-            vmem(p1.shape, BF16),
-            dma((6,)), dma((sources,)), dma, dma, dma, dma, dma((rows,)), dma((rows,)),
+            dma((6,)), dma, dma, dma, dma, dma((rows,)), dma((rows,)),
         ],
         compiler_params=pltpu.CompilerParams(
-            collective_id=0, has_side_effects=True, vmem_limit_bytes=60 * 2**20
+            collective_id=0, has_side_effects=True, vmem_limit_bytes=50 * 2**20
         ),
-    )(p1, p2, p3, ws, we, jnp.asarray(make_table(size, samples)))
+    )(*(pltpu.with_memory_space_constraint(a, pltpu.HBM) for a in (p1, p2, p3, ws, we, table)))
+    return pl.pallas_call(
+        functools.partial(finish, size),
+        out_shape=jax.ShapeDtypeStruct(p1.shape, BF16),
+        in_specs=[pl.BlockSpec(memory_space=pltpu.VMEM)] * 2,
+        out_specs=pl.BlockSpec(memory_space=pltpu.HBM),
+        scratch_shapes=[vmem(p1.shape, BF16), dma((sources,))],
+        compiler_params=pltpu.CompilerParams(vmem_limit_bytes=16 * 2**20),
+    )(lines, kept)
 
 
 def solution(mesh):

time: 221 us -> 218 us (0.986)
  local copies, waits for them, and re-layouts: 3.05 us -> 0 us
    unnamed x1 -> x0, local copies, waits for them, and re-layouts: 3.05 us -> none
    pallas_call x1 -> x2, Pallas kernels: 218 us -> 218 us  [the longest x1 216 us: on_device(): pl.pallas_call(functools.partial(kernel, size), out_shape=(jax.ShapeDtype...]
where the time goes in v2:
time: 218 us
  Pallas kernels  218 us (100%)
    pallas_call x1, Pallas kernels, on_device(): pl.pallas_call(functools.partial(kernel, size), out_shape=(jax.ShapeDtype...  216 us

profile of v2, /device:TPU:33, one launch (start us, length us, event | category | flops | bytes accessed | tf_op | source)
XLA Modules:
  0.0 217.8 jit_solution(3684634478793617832)
XLA Ops:
  0.0 216.1 %shard_map.64 = (f32[4,1024,128]{2,1,0:T(8,128)S(1)}, bf16[256,512]{1,0:T(8,128)(2,1)S(1)}) custom-call(bf16[4,512,512]{2,1,0:T(8,128)(2,1)} %p1.1, bf16[4,512,512]{2,1,0:T(8,128)(2,1)} %p2.1, bf16[4,512,512]{2,1,0:T(8,128)(2,1)} %p3.1, s32[3,4,512]{2,1,0:T(4,128)} %ws.1, s32[3,4,512]{2,1,0:T(4,128)} %we.1, bf16[256,512]{1,0:T(8,128)(2,1)} %constant.2.clone.tab_hbm), custom_call_target="tpu_custom_call" | custom-call | tf_op jit(solution)/shard_map/pallas_call | solution.py:248
  216.1 1.7 shard_map.65

commit v3 on v2

--- a/solution.py
+++ b/solution.py
@@ -30,7 +30,7 @@
 def kernel(
     size, p1, p2, p3, ws, we, tab_hbm, m32, tab,
     inp, wsv, wev, a32, b32, s23, s1, r23, r1, xm, ym, zm, w, o, m,
-    in_sem, ssem23, ssem1, ssemo, rsem23, rsem1, rsemo,
+    in_sem, ssem23, ssem1, ssemo, rsem23, rsem1, rsemo, up, last_in,
 ):
     me = lax.axis_index("freq")
     group = lax.axis_index("groups")
@@ -42,8 +42,31 @@
 
     barrier = pltpu.get_barrier_semaphore()
 
-    def greet(k, carry):
-        pl.semaphore_signal(barrier, inc=1, device_id=(group, (me + k) % size), device_id_type=MESH)
+    def greet(turn, carry):
+        mate = z * ROW + (xc + turn) % ROW
+
+        @pl.when(mate != 0)
+        def _():
+            pl.semaphore_signal(barrier, inc=1, device_id=(group, mate), device_id_type=MESH)
+
+        return carry
+
+    def report(below, carry):
+        target = below * ROW + xc
+
+        @pl.when(target != 0)
+        def _():
+            pl.semaphore_signal(up.at[z], inc=1, device_id=(group, target), device_id_type=MESH)
+
+        return carry
+
+    def announce(turn, carry):
+        mate = z * ROW + (xc + turn) % ROW
+        pl.semaphore_signal(last_in, inc=1, device_id=(group, mate), device_id_type=MESH)
+        return carry
+
+    def announce_row(row, carry):
+        pl.semaphore_signal(last_in, inc=1, device_id=(group, row * ROW), device_id_type=MESH)
         return carry
 
     loads = [
@@ -56,7 +79,26 @@
     ]
     for load in loads:
         load.start()
-    lax.fori_loop(1, size, greet, 0)
+
+    @pl.when(me != 0)
+    def _():
+        lax.fori_loop(1, ROW, greet, 0)
+        pl.semaphore_wait(barrier, ROW - 2 + 2 * jnp.minimum(z, 1))
+
+        @pl.when(z < rows - 1)
+        def _():
+            pl.semaphore_signal(barrier, inc=1, device_id=(group, me + ROW), device_id_type=MESH)
+
+        @pl.when(me == 1)
+        def _():
+            pl.semaphore_signal(barrier, inc=1, device_id=(group, ROW), device_id_type=MESH)
+
+        @pl.when(me == size - ROW)
+        def _():
+            pl.semaphore_signal(barrier, inc=1, device_id=(group, 0), device_id_type=MESH)
+
+        lax.fori_loop(0, z, report, 0)
+
     for load in loads[:3]:
         load.wait()
 
@@ -91,23 +133,52 @@
     loads[4].wait()
     spectra(2, a32, per, 2 * per)
 
-    def round23(i, carry):
-        at = pl.multiple_of(i * ROW, ROW)
-        lines = pl.ds(pl.multiple_of(i * ROW * 2 * per, ROW * 2 * per), ROW * 2 * per)
+    def partner_row(block):
+        return (z + shift_of(block) + rows) % rows
+
+    def round23(row):
+        lines = pl.ds(pl.multiple_of(row * ROW * 2 * per, ROW * 2 * per), ROW * 2 * per)
         for q in range(receivers // LANES):
             piece = a32[q, lines, :].reshape(ROW, 2 * per, LANES)
-            s23[pl.ds(at, ROW), :, q * LANES : (q + 1) * LANES] = piece.astype(BF16)
-        return carry
-
-    lax.fori_loop(0, rows, round23, 0)
-    pl.semaphore_wait(barrier, size - 1)
-
-    def send23(block, dst):
+            s23[pl.ds(pl.multiple_of(row * ROW, ROW), ROW), :, q * LANES : (q + 1) * LANES] = piece.astype(BF16)
+
+    def send23_to(dst):
         pltpu.make_async_remote_copy(
             s23.at[dst], r23.at[me], ssem23, rsem23, device_id=(group, dst), device_id_type=MESH
         ).start()
 
-    each_partner(send23)
+    def send23(row):
+        def step(turn, carry):
+            dst = row * ROW + (xc + turn) % ROW
+
+            @pl.when((dst != me) & (dst != 0))
+            def _():
+                send23_to(dst)
+
+            return carry
+
+        lax.fori_loop(0, ROW, step, 0)
+
+    round23(z)
+
+    @pl.when(me == 0)
+    def _():
+        pl.semaphore_wait(barrier, 1)
+        lax.fori_loop(1, rows, announce_row, 0)
+        lax.fori_loop(1, ROW, announce, 0)
+
+    def early(block, carry):
+        @pl.when(block < rows - 1)
+        def _():
+            round23(partner_row((block + 1) % rows))
+
+        @pl.when(partner_row(block) <= z)
+        def _():
+            send23(partner_row(block))
+
+        return carry
+
+    lax.fori_loop(0, rows, early, 0)
     r23[me] = s23[me]
 
     loads[5].wait()
@@ -122,6 +193,26 @@
         return carry
 
     lax.fori_loop(0, rows, round1, 0)
+
+    def late(row, carry):
+        @pl.when(me != 0)
+        def _():
+            pl.semaphore_wait(up.at[row], 1)
+
+        send23(row)
+        return carry
+
+    lax.fori_loop(z + 1, rows, late, 0)
+
+    @pl.when(me != 0)
+    def _():
+        pl.semaphore_wait(last_in, 1)
+
+        @pl.when(xc == 0)
+        def _():
+            lax.fori_loop(1, ROW, announce, 0)
+
+        send23_to(0)
 
     def send1(block, dst):
         pltpu.make_async_remote_copy(
@@ -270,6 +361,7 @@
             vmem((size, per, receivers), BF16),
             vmem((size, per, receivers), BF16),
             dma((6,)), dma, dma, dma, dma, dma((rows,)), dma((rows,)),
+            pltpu.SemaphoreType.REGULAR((rows,)), pltpu.SemaphoreType.REGULAR,
         ],
         compiler_params=pltpu.CompilerParams(
             collective_id=0, has_side_effects=True, vmem_limit_bytes=50 * 2**20

time: 218 us -> 210 us (0.963); the launches traced: 218 us -> 206 us
  Pallas kernels: 218 us -> 206 us
    pallas_call x1, Pallas kernels: 216 us -> 204 us  [on_device(): pl.pallas_call(functools.partial(kernel, size), out_shape=(jax.ShapeDtype...]
where the time goes in v3:
time: 210 us; the launch traced here: 206 us
  Pallas kernels  206 us (98%)
    pallas_call x1, Pallas kernels, on_device(): pl.pallas_call(functools.partial(kernel, size), out_shape=(jax.ShapeDtype...  204 us

profile of v3, /device:TPU:33, one launch (start us, length us, event | category | flops | bytes accessed | tf_op | source)
XLA Modules:
  0.0 205.6 jit_solution(4887556885847035590)
XLA Ops:
  0.0 203.9 %shard_map.64 = (f32[4,1024,128]{2,1,0:T(8,128)S(1)}, bf16[256,512]{1,0:T(8,128)(2,1)S(1)}) custom-call(bf16[4,512,512]{2,1,0:T(8,128)(2,1)} %p1.1, bf16[4,512,512]{2,1,0:T(8,128)(2,1)} %p2.1, bf16[4,512,512]{2,1,0:T(8,128)(2,1)} %p3.1, s32[3,4,512]{2,1,0:T(4,128)} %ws.1, s32[3,4,512]{2,1,0:T(4,128)} %we.1, bf16[256,512]{1,0:T(8,128)(2,1)} %constant.2.clone.tab_hbm), custom_call_target="tpu_custom_call" | custom-call | tf_op jit(solution)/shard_map/pallas_call | solution.py:339
  203.9 1.7 shard_map.65

commit v4 on v3

--- a/solution.py
+++ b/solution.py
@@ -251,7 +251,10 @@
     lax.fori_loop(0, receivers // LANES, weigh, 0)
     scale1 = np.float32(1.0 / np.sqrt(receivers))
 
-    def multiply(block, carry):
+    def multiply(i, carry):
+        gap = (z - i + rows) % rows
+        block = jnp.where(gap <= rows // 2, 2 * gap - 1, 2 * (rows - gap))
+        block = jnp.where(gap == 0, 0, block)
         came = ((z - shift_of(block) + rows) % rows) * ROW
 
         @pl.when(block == 0)

time: 210 us -> 215 us (1.024); the launches traced: 206 us -> 215 us
  Pallas kernels: 206 us -> 215 us
    pallas_call x1, Pallas kernels: 204 us -> 213 us  [on_device(): pl.pallas_call(functools.partial(kernel, size), out_shape=(jax.ShapeDtype...]
where the time goes in v4:
time: 215 us
  Pallas kernels  215 us (100%)
    pallas_call x1, Pallas kernels, on_device(): pl.pallas_call(functools.partial(kernel, size), out_shape=(jax.ShapeDtype...  213 us

profile of v4, /device:TPU:33, one launch (start us, length us, event | category | flops | bytes accessed | tf_op | source)
XLA Modules:
  0.0 214.9 jit_solution(9649124605220173394)
XLA Ops:
  0.0 213.2 %shard_map.64 = (f32[4,1024,128]{2,1,0:T(8,128)S(1)}, bf16[256,512]{1,0:T(8,128)(2,1)S(1)}) custom-call(bf16[4,512,512]{2,1,0:T(8,128)(2,1)} %p1.1, bf16[4,512,512]{2,1,0:T(8,128)(2,1)} %p2.1, bf16[4,512,512]{2,1,0:T(8,128)(2,1)} %p3.1, s32[3,4,512]{2,1,0:T(4,128)} %ws.1, s32[3,4,512]{2,1,0:T(4,128)} %we.1, bf16[256,512]{1,0:T(8,128)(2,1)} %constant.2.clone.tab_hbm), custom_call_target="tpu_custom_call" | custom-call | tf_op jit(solution)/shard_map/pallas_call | solution.py:342
  213.3 1.7 shard_map.65
